TPU v7x, 512 devices: a whole 4x8x8 slice. The times are simulated.
512 devices in a mesh: group: 2 (over core), dp: 64 (over y, x, z_hi), mp: 4 (over z_lo).
Axes of the slice: x: 4, y: 8, z: 8 (z_hi: 2, z_lo: 4; z = z_hi * 4 + z_lo), core: 2. Of those that a mesh axis runs over, the one named last changes fastest.
Arguments:
- x_arrive: bfloat16 [256, 256, 1152], P(('group', 'dp')), may hold values from -6 to 6
- cond_first: int32 [128], P(('group', 'dp')), may hold values 0 or 1
- labels: int32 [128], P(('group', 'dp')), may hold values from 0 to 999
- step_ids: int32 [128], P(('group', 'dp')), may hold values from 0 to 999
- guidance: float32 [1], replicated, may hold values from 2 to 6
- time_table: bfloat16 [1000, 1152], P(None, 'mp'), may hold values from -6 to 6
- class_table: bfloat16 [1001, 1152], P(None, 'mp'), may hold values from -6 to 6
- ada_weight: bfloat16 [1152, 6912], P('mp', 'dp'), may hold values from -0.1875 to 0.1875
- final_ada: bfloat16 [1152, 2304], P('mp'), may hold values from -0.1875 to 0.1875
- qkv_weight: bfloat16 [3, 1152, 1152], P(None, 'dp', 'mp'), may hold values from -2 to 2
- proj_weight: bfloat16 [1152, 1152], P('mp', 'dp'), may hold values from -0.1875 to 0.1875
- fc1_weight: bfloat16 [1152, 4608], P('dp', 'mp'), may hold values from -0.1875 to 0.1875
- fc2_weight: bfloat16 [4608, 1152], P('mp', 'dp'), may hold values from -0.09375 to 0.09375
- out_weight: bfloat16 [1152, 16], replicated, may hold values from -0.1875 to 0.1875
Outputs:
- guided: float32 [128, 4096], P(('group', 'dp'), 'mp')
All inputs are finite; a program needn't handle non-finite values. No bound on the sum of `cond_first` on one device may be relied on, other than what follows from the above.
Results may differ from a plain program's by a relative error of at most 0.025.
Values may be sent and summed in bfloat16 or wider, within the bound.
No kernel may reach another device: no remote copies, remote signals or barrier semaphores. Data moves between devices by JAX's collectives and lax.ppermute only.
A program may use at most 64 MiB of HBM per device.

v0:
```python
import jax
import jax.numpy as jnp
from jax import lax
from jax.sharding import Mesh
from jax.sharding import PartitionSpec as P

HEADS = 16
CLASSES = 1000
DP = ("dp_0", "dp_1", "dp_2")
GROUP_DP = ("group", "dp_0", "dp_1", "dp_2")


def from_everyone(x, axis):
    size = lax.axis_size(axis)
    return lax.all_to_all(jnp.broadcast_to(x[None], (size, *x.shape)), axis, 0, 0, tiled=True)


def laid_out(pieces, dim):
    pieces = jnp.moveaxis(pieces, 0, dim)
    shape = pieces.shape
    return pieces.reshape(*shape[:dim], shape[dim] * shape[dim + 1], *shape[dim + 2 :])


def collect(x, axis, dim):
    pieces = from_everyone(x, axis)
    return laid_out(pieces, dim)


def of_everyone(x, axis):
    everything = from_everyone(x, axis)
    return jnp.sum(everything.astype(jnp.float32), axis=0)


def gathered_by_axis(x, axes, dim):
    for axis in reversed(axes):
        x = lax.all_gather(x, axis, axis=dim, tiled=True)
    return x


def cut_along(x, dim, size):
    shape = x.shape
    pieces = x.reshape(*shape[:dim], size, shape[dim] // size, *shape[dim + 1 :])
    return jnp.moveaxis(pieces, dim, 0)


def sum_at_owner(x, axis, dim):
    size = lax.axis_size(axis)
    pieces = lax.all_to_all(cut_along(x, dim, size), axis, 0, 0, tiled=True)
    return jnp.sum(pieces.astype(jnp.float32), axis=0)


def layer_norm(values):
    mean = jnp.mean(values, axis=-1, keepdims=True)
    centred = values - mean
    spread = jnp.mean(centred * centred, axis=-1, keepdims=True)
    return centred * lax.rsqrt(spread + 1e-06)


def on_device(
    x_arrive,
    cond_first,
    labels,
    step_ids,
    guidance,
    time_table,
    class_table,
    ada_weight,
    final_ada,
    qkv_weight,
    proj_weight,
    fc1_weight,
    fc2_weight,
    out_weight,
):
    pair_count = labels.shape[0]
    tokens = x_arrive.shape[1]
    width = x_arrive.shape[2]
    image_count = 2 * pair_count
    row_count = image_count * tokens
    split_rows = x_arrive.reshape(pair_count, 2, tokens, width)
    first = (cond_first == 1)[:, None, None]
    cond_rows = jnp.where(first, split_rows[:, 0], split_rows[:, 1])
    uncond_rows = jnp.where(first, split_rows[:, 1], split_rows[:, 0])
    x_sides = jnp.stack([cond_rows, uncond_rows])
    time_part = jnp.take(time_table, step_ids, axis=0).astype(jnp.float32)
    class_part = jnp.take(class_table, labels, axis=0).astype(jnp.float32)
    null_part = class_table[CLASSES].astype(jnp.float32)[None, :]
    emb_sides = time_part[None] + jnp.stack([class_part, null_part])
    act_sides = jax.nn.silu(emb_sides).astype(jnp.bfloat16)
    images, acts = (x_sides, act_sides)
    images = images.reshape(image_count, tokens, width)
    acts = acts.reshape(image_count, act_sides.shape[2])
    partial_final = jnp.dot(acts, final_ada, preferred_element_type=jnp.float32)
    every_act = collect(acts, DP, 0)
    column_part = jnp.dot(every_act, ada_weight, preferred_element_type=jnp.float32)
    summed, fmods = (
        of_everyone(column_part.astype(jnp.bfloat16), "mp").astype(jnp.float32),
        of_everyone(partial_final.astype(jnp.bfloat16), "mp").astype(jnp.float32),
    )
    mods = lax.all_to_all(
        summed.astype(jnp.bfloat16), DP, split_axis=0, concat_axis=1, tiled=True
    ).astype(summed.dtype)
    shift_a, scale_a, gate_a, shift_m, scale_m, gate_m = jnp.split(mods, 6, axis=1)
    shift_f, scale_f = jnp.split(fmods, 2, axis=1)
    images_f = images.astype(jnp.float32)
    hidden = (layer_norm(images_f) * (1.0 + scale_a[:, None]) + shift_a[:, None]).astype(
        jnp.bfloat16
    )
    hidden = hidden.reshape(row_count, width)
    quarter = qkv_weight.shape[2]
    head_dim = width // HEADS
    local_heads = quarter // head_dim
    columns = hidden
    qkv = jnp.einsum(
        "rd,kdc->krc",
        columns,
        lax.all_gather(qkv_weight, DP, axis=1, tiled=True),
        preferred_element_type=jnp.float32,
    ).astype(jnp.bfloat16)
    query = qkv[0].reshape(image_count, tokens, local_heads, head_dim)
    keys = qkv[1].reshape(image_count, tokens, local_heads, head_dim)
    values = qkv[2].reshape(image_count, tokens, local_heads, head_dim)
    scores = jnp.einsum(
        "bqhe,bkhe->bhqk", query, keys, preferred_element_type=jnp.float32
    ) * head_dim ** (-0.5)
    probs = jax.nn.softmax(scores, axis=-1).astype(jnp.bfloat16)
    mixed = jnp.einsum("bhqk,bkhe->bqhe", probs, values, preferred_element_type=jnp.float32).astype(
        jnp.bfloat16
    )
    mixed = mixed.reshape(row_count, quarter)
    attn_part = jnp.dot(mixed, collect(proj_weight, DP, 1), preferred_element_type=jnp.float32)
    attn = (
        lax.psum(attn_part.astype(jnp.bfloat16), "mp")
        .astype(jnp.float32)
        .reshape(image_count, tokens, width)
    )
    first_sum = images_f + gate_a[:, None] * attn
    hidden_two = (layer_norm(first_sum) * (1.0 + scale_m[:, None]) + shift_m[:, None]).astype(
        jnp.bfloat16
    )
    hidden_two = hidden_two.reshape(row_count, width)
    ff_quarter = fc1_weight.shape[1]
    columns = hidden_two
    up = jnp.dot(columns, gathered_by_axis(fc1_weight, DP, 0), preferred_element_type=jnp.float32)
    gelu_h = (
        jax.nn.gelu(up, approximate=True)
        .astype(jnp.bfloat16)
        .reshape(image_count, tokens, ff_quarter)
    )
    down_full = gathered_by_axis(fc2_weight, DP, 1)
    token_share = tokens // lax.axis_size("mp")
    mlp = sum_at_owner(
        jnp.einsum("btf,fd->tbd", gelu_h, down_full, preferred_element_type=jnp.float32).astype(
            jnp.bfloat16
        ),
        "mp",
        0,
    )
    token_start = lax.axis_index("mp") * token_share
    own_first = lax.dynamic_slice_in_dim(first_sum, token_start, token_share, 1).transpose(1, 0, 2)
    second_sum = own_first + gate_m[None] * mlp
    fin = (layer_norm(second_sum) * (1.0 + scale_f[None]) + shift_f[None]).astype(jnp.bfloat16)
    noise = jnp.einsum("tbd,do->bto", fin, out_weight, preferred_element_type=jnp.float32)
    noise = noise.reshape(2, pair_count, token_share * out_weight.shape[1])
    return noise[1] + guidance[0] * (noise[0] - noise[1])


def solution(mesh):
    torus = Mesh(
        mesh.devices.reshape(mesh.shape["group"], 8, 4, 2, mesh.shape["mp"]),
        ("group", "dp_0", "dp_1", "dp_2", "mp"),
    )
    placed = (
        P(GROUP_DP, None, None),
        P(GROUP_DP),
        P(GROUP_DP),
        P(GROUP_DP),
        P(),
        P(None, "mp"),
        P(None, "mp"),
        P("mp", DP),
        P("mp", None),
        P(None, DP, "mp"),
        P("mp", DP),
        P(DP, "mp"),
        P("mp", DP),
        P(),
    )
    return jax.shard_map(
        on_device, mesh=torus, in_specs=placed, out_specs=P(GROUP_DP, "mp"), check_vma=False
    )
```

profile of v0, /device:TPU:4, one launch (start us, length us, event | category | flops | bytes accessed | tf_op | source)
XLA Modules:
  0.0 341.8 jit_solution(6708045404015547400)
XLA Ops:
  7.4 1.6 copy.106
  13.9 19.2 %all-to-all-start = ((bf16[64,2,288]{2,1,0:T(2,128)(2,1)}), bf16[64,2,288]{2,1,0:T(2,128)(2,1)S(1)}, u32[]{:S(2)}, u32[]{:S(2)}) async-start(bf16[64,2,288]{2,1,0:T(2,128)(2,1)} %broadcast_in_dim.50), calls=%async_computation | async-start | bytes 196608 | tf_op jit(solution)/shard_map/all_to_all | solution.py:15
  33.8 12.4 %all-to-all-done = bf16[64,2,288]{2,1,0:T(2,128)(2,1)S(1)} async-done(((bf16[64,2,288]{2,1,0:T(2,128)(2,1)}), bf16[64,2,288]{2,1,0:T(2,128)(2,1)S(1)}, u32[]{:S(2)}, u32[]{:S(2)}) %all-to-all-start) | async-done | bytes 73760 | tf_op jit(solution)/shard_map/all_to_all | solution.py:15
  48.1 4.5 %all-to-all-start.1 = ((bf16[4,128,108]{1,2,0:T(8,128)(2,1)}), bf16[4,128,108]{1,2,0:T(8,128)(2,1)S(1)}, u32[]{:S(2)}, u32[]{:S(2)}) async-start(bf16[4,128,108]{1,2,0:T(8,128)(2,1)} %broadcast_in_dim.84), calls=%async_computation.1 | async-start | bytes 229376 | tf_op jit(solution)/shard_map/all_to_all | solution.py:15
  53.9 4.5 %all-to-all-done.1 = bf16[4,128,108]{1,2,0:T(8,128)(2,1)S(1)} async-done(((bf16[4,128,108]{1,2,0:T(8,128)(2,1)}), bf16[4,128,108]{1,2,0:T(8,128)(2,1)S(1)}, u32[]{:S(2)}, u32[]{:S(2)}) %all-to-all-start.1) | async-done | bytes 110624 | tf_op jit(solution)/shard_map/all_to_all | solution.py:15
  59.2 6.2 %all-to-all-start.2 = ((bf16[64,2,108]{2,1,0:T(2,128)(2,1)}), bf16[64,2,108]{2,1,0:T(2,128)(2,1)S(1)}, u32[]{:S(2)}, u32[]{:S(2)}) async-start(bf16[64,2,108]{2,1,0:T(2,128)(2,1)} %bitcast.7), calls=%async_computation.2 | async-start | bytes 65536 | tf_op jit(solution)/shard_map/all_to_all | solution.py:100
  65.6 12.4 %all-to-all-done.2 = bf16[64,2,108]{2,1,0:T(2,128)(2,1)S(1)} async-done(((bf16[64,2,108]{2,1,0:T(2,128)(2,1)}), bf16[64,2,108]{2,1,0:T(2,128)(2,1)S(1)}, u32[]{:S(2)}, u32[]{:S(2)}) %all-to-all-start.2) | async-done | bytes 27680 | tf_op jit(solution)/shard_map/all_to_all | solution.py:100
  79.1 7.2 %all-to-all-start.3 = ((bf16[64,288,18]{1,2,0:T(8,128)(2,1)}), bf16[64,288,18]{1,2,0:T(8,128)(2,1)}, u32[]{:S(2)}, u32[]{:S(2)}) async-start(bf16[64,288,18]{1,2,0:T(8,128)(2,1)} %broadcast_in_dim.85), calls=%async_computation.3 | async-start | bytes 2359296 | tf_op jit(solution)/shard_map/all_to_all | solution.py:15
  87.1 1.7 fusion.16
  88.8 30.6 %all-to-all-done.3 = bf16[64,288,18]{1,2,0:T(8,128)(2,1)} async-done(((bf16[64,288,18]{1,2,0:T(8,128)(2,1)}), bf16[64,288,18]{1,2,0:T(8,128)(2,1)}, u32[]{:S(2)}, u32[]{:S(2)}) %all-to-all-start.3) | async-done | bytes 663584 | tf_op jit(solution)/shard_map/all_to_all | solution.py:15
  119.4 1.6 reshape.262
  121.0 51.8 %all-gather.8.cloned.1.call-done = bf16[3,1152,288]{2,0,1:T(4,128)(2,1)} async-done(((bf16[3,18,288]{2,0,1:T(4,128)(2,1)}), bf16[3,1152,288]{2,0,1:T(4,128)(2,1)}) %all-gather.8.cloned.1.call-update) | async-done | bytes 1990672 | tf_op jit(solution)/shard_map/all_gather | solution.py:117
  172.8 3.7 %fusion.26 = bf16[3,512,288]{1,2,0:T(8,128)(2,1)S(1)} fusion(bf16[3,1152,288]{2,0,1:T(4,128)(2,1)} %all-gather.8.cloned.1.call-done, bf16[512,1152]{1,0:T(8,128)(2,1)} %fusion.16), kind=kOutput, calls=%fused_computation.41 | convolution fusion | flops 1019658240 | bytes 4055040 | tf_op jit(solution)/shard_map/rd,kdc->krc/dot_general | solution.py:114
  177.5 1.7 reshape_squeeze.10
  179.3 1.7 reshape_squeeze.11
  181.0 1.8 reshape_squeeze.9
  182.8 3.2 fusion.65
  186.0 2.0 fusion.30
  188.4 2.0 convolution_convert_fusion.2
  190.4 9.3 %all-gather = bf16[2,18,1152]{2,1,0:T(8,128)(2,1)S(1)} all-gather(bf16[1,18,1152]{2,1,0:T(8,128)(2,1)S(1)} %bitcast.125), channel_id=1, replica_groups=mesh['group'=2,'dp_0'=8,'dp_1'=4,'dp_2'=2,'mp'=4] {'dp_2'}, dimensions={0}, use_global_device_ids=true | all-gather | bytes 124416 | tf_op jit(solution)/shard_map/all_gather | solution.py:36
  199.8 11.3 %all-gather.1 = bf16[4,36,1152]{2,1,0:T(8,128)(2,1)S(1)} all-gather(bf16[1,36,1152]{2,1,0:T(8,128)(2,1)S(1)} %reshape.323), channel_id=1, replica_groups=mesh['group'=2,'dp_0'=8,'dp_1'=4,'dp_2'=2,'mp'=4] {'dp_1'}, dimensions={0}, use_global_device_ids=true | all-gather | bytes 414720 | tf_op jit(solution)/shard_map/all_gather | solution.py:36
  211.9 10.3 %all-gather.2 = bf16[2,18,1152]{2,1,0:T(8,128)(2,1)S(1)} all-gather(bf16[1,18,1152]{2,1,0:T(8,128)(2,1)S(1)} %bitcast.126), channel_id=1, replica_groups=mesh['group'=2,'dp_0'=8,'dp_1'=4,'dp_2'=2,'mp'=4] {'dp_2'}, dimensions={0}, use_global_device_ids=true | all-gather | bytes 124416 | tf_op jit(solution)/shard_map/all_gather | solution.py:36
  222.2 12.4 %all-gather.3 = bf16[4,36,1152]{2,1,0:T(8,128)(2,1)S(1)} all-gather(bf16[1,36,1152]{2,1,0:T(8,128)(2,1)S(1)} %reshape.327), channel_id=1, replica_groups=mesh['group'=2,'dp_0'=8,'dp_1'=4,'dp_2'=2,'mp'=4] {'dp_1'}, dimensions={0}, use_global_device_ids=true | all-gather | bytes 414720 | tf_op jit(solution)/shard_map/all_gather | solution.py:36
  236.5 3.4 %all-to-all-start.5 = ((bf16[4,2,2304]{2,1,0:T(2,128)(2,1)}), bf16[4,2,2304]{2,1,0:T(2,128)(2,1)S(1)}, u32[]{:S(2)}, u32[]{:S(2)}) async-start(bf16[4,2,2304]{2,1,0:T(2,128)(2,1)} %broadcast_in_dim.86), calls=%async_computation.5 | async-start | bytes 73728 | tf_op jit(solution)/shard_map/all_to_all | solution.py:15
  240.0 21.1 %all-reduce.2.cloned.1.call-done = bf16[512,1152]{1,0:T(8,128)(2,1)} async-done(((bf16[512,1152]{1,0:T(8,128)(2,1)}), bf16[512,1152]{1,0:T(8,128)(2,1)}) %all-reduce.2.cloned.1.call-update) | async-done | bytes 1179664 | tf_op jit(solution)/shard_map/psum | solution.py:133
  261.1 1.7 fusion.60
  264.9 2.0 fusion.12
  266.9 4.0 %fusion.11 = bf16[512,1152]{1,0:T(8,128)(2,1)S(1)} fusion(bf16[512,1152]{1,0:T(8,128)(2,1)} %fusion.12, bf16[1152,1152]{1,0:T(8,128)(2,1)} %all-gather.10.cloned.1.call-done), kind=kOutput, calls=%fused_computation.15 | convolution fusion | flops 1364262912 | bytes 5013504 | tf_op jit(solution)/shard_map/dot_general | solution.py:144
  271.0 25.5 %all-gather.12.cloned.1.call-done = bf16[1152,1152]{0,1:T(8,128)(2,1)} async-done(((bf16[1152,144]{0,1:T(8,128)(2,1)}), bf16[1152,1152]{0,1:T(8,128)(2,1)}) %all-gather.12.cloned.1.call-update) | async-done | bytes 2654224 | tf_op jit(solution)/shard_map/all_gather | solution.py:36
  296.4 3.6 %convolution_convert_fusion.1 = bf16[2,256,1152]{2,1,0:T(8,128)(2,1)S(1)} fusion(bf16[2,256,1152]{2,1,0:T(8,128)(2,1)S(1)} %bitcast.131, bf16[1152,1152]{0,1:T(8,128)(2,1)} %all-gather.12.cloned.1.call-done), kind=kOutput, calls=%fused_computation.3 | convolution fusion | flops 1359544320 | bytes 5013504 | tf_op jit(solution)/shard_map/btf,fd->tbd/dot_general | solution.py:153
  301.2 4.8 %all-to-all-start.4 = ((bf16[4,64,2,1152]{3,1,2,0:T(8,128)(2,1)}), bf16[4,64,2,1152]{3,1,2,0:T(8,128)(2,1)S(1)}, u32[]{:S(2)}, u32[]{:S(2)}) async-start(bf16[4,64,2,1152]{3,1,2,0:T(8,128)(2,1)} %copy.113), calls=%async_computation.4 | async-start | bytes 2359296 | tf_op jit(solution)/shard_map/all_to_all | solution.py:48
  306.7 24.8 %all-to-all-done.4 = bf16[4,64,2,1152]{3,1,2,0:T(8,128)(2,1)S(1)} async-done(((bf16[4,64,2,1152]{3,1,2,0:T(8,128)(2,1)}), bf16[4,64,2,1152]{3,1,2,0:T(8,128)(2,1)S(1)}, u32[]{:S(2)}, u32[]{:S(2)}) %all-to-all-start.4) | async-done | bytes 1179680 | tf_op jit(solution)/shard_map/all_to_all | solution.py:48
  (83 shorter events, 19.9 us)
Async XLA Ops:
  7.4 228.2 %copy-start = (bf16[288,2304]{1,0:T(8,128)(2,1)S(1)}, bf16[288,2304]{1,0:T(8,128)(2,1)}, u32[]{:S(2)}) copy-start(bf16[288,2304]{1,0:T(8,128)(2,1)} %param.22) | copy-start | bytes 3981316
  7.4 165.5 %all-gather.8.cloned.1.call-start = ((), (), s32[]{:S(2)}) async-start(), calls=%async_computation.6 | async-start | bytes 3594240 | tf_op jit(solution)/shard_map/all_gather | solution.py:117
  12.7 0.6 copy-start.6
  13.9 64.1 %copy-start.5 = (bf16[288,18]{0,1:T(8,128)(2,1)S(1)}, bf16[288,18]{0,1:T(8,128)(2,1)}, u32[]{:S(2)}) copy-start(bf16[288,18]{0,1:T(8,128)(2,1)} %param.24) | copy-start | bytes 31108
  13.9 32.3 %all-to-all-start = ((bf16[64,2,288]{2,1,0:T(2,128)(2,1)}), bf16[64,2,288]{2,1,0:T(2,128)(2,1)S(1)}, u32[]{:S(2)}, u32[]{:S(2)}) async-start(bf16[64,2,288]{2,1,0:T(2,128)(2,1)} %broadcast_in_dim.50), calls=%async_computation | async-start | bytes 196608 | tf_op jit(solution)/shard_map/all_to_all | solution.py:15
  48.1 10.4 %all-to-all-start.1 = ((bf16[4,128,108]{1,2,0:T(8,128)(2,1)}), bf16[4,128,108]{1,2,0:T(8,128)(2,1)S(1)}, u32[]{:S(2)}, u32[]{:S(2)}) async-start(bf16[4,128,108]{1,2,0:T(8,128)(2,1)} %broadcast_in_dim.84), calls=%async_computation.1 | async-start | bytes 229376 | tf_op jit(solution)/shard_map/all_to_all | solution.py:15
  59.2 18.8 %all-to-all-start.2 = ((bf16[64,2,108]{2,1,0:T(2,128)(2,1)}), bf16[64,2,108]{2,1,0:T(2,128)(2,1)S(1)}, u32[]{:S(2)}, u32[]{:S(2)}) async-start(bf16[64,2,108]{2,1,0:T(2,128)(2,1)} %bitcast.7), calls=%async_computation.2 | async-start | bytes 65536 | tf_op jit(solution)/shard_map/all_to_all | solution.py:100
  79.1 40.3 %all-to-all-start.3 = ((bf16[64,288,18]{1,2,0:T(8,128)(2,1)}), bf16[64,288,18]{1,2,0:T(8,128)(2,1)}, u32[]{:S(2)}, u32[]{:S(2)}) async-start(bf16[64,288,18]{1,2,0:T(8,128)(2,1)} %broadcast_in_dim.85), calls=%async_computation.3 | async-start | bytes 2359296 | tf_op jit(solution)/shard_map/all_to_all | solution.py:15
  86.3 174.8 %all-reduce.2.cloned.1.call-start = ((), (), s32[]{:S(2)}) async-start(), calls=%async_computation.7 | async-start | bytes 2359296 | tf_op jit(solution)/shard_map/psum | solution.py:133
  188.0 2.4 copy-start.3
  188.4 23.6 %copy-start.4 = (bf16[1152,18]{0,1:T(8,128)(2,1)S(1)}, bf16[1152,18]{0,1:T(8,128)(2,1)}, u32[]{:S(2)}) copy-start(bf16[1152,18]{0,1:T(8,128)(2,1)} %param.26) | copy-start | bytes 124420
  190.3 45.2 %copy-start.7 = (bf16[2,288]{1,0:T(2,128)(2,1)S(1)}, bf16[2,288]{1,0:T(2,128)(2,1)}, u32[]{:S(2)}) copy-start(bf16[2,288]{1,0:T(2,128)(2,1)} %copy-done.6) | copy-start | bytes 3460
  190.4 76.6 %all-gather.10.cloned.1.call-start = ((), (), s32[]{:S(2)}) async-start(), calls=%async_computation.8 | async-start | bytes 2985984 | tf_op jit(solution)/shard_map/all_gather | solution.py:36
  211.9 84.6 %all-gather.12.cloned.1.call-start = ((), (), s32[]{:S(2)}) async-start(), calls=%async_computation.9 | async-start | bytes 2985984 | tf_op jit(solution)/shard_map/all_gather | solution.py:36
  236.5 64.7 %all-to-all-start.5 = ((bf16[4,2,2304]{2,1,0:T(2,128)(2,1)}), bf16[4,2,2304]{2,1,0:T(2,128)(2,1)S(1)}, u32[]{:S(2)}, u32[]{:S(2)}) async-start(bf16[4,2,2304]{2,1,0:T(2,128)(2,1)} %broadcast_in_dim.86), calls=%async_computation.5 | async-start | bytes 73728 | tf_op jit(solution)/shard_map/all_to_all | solution.py:15
  262.8 1.4 copy-start.1
  262.8 2.1 copy-start.2
  301.2 30.3 %all-to-all-start.4 = ((bf16[4,64,2,1152]{3,1,2,0:T(8,128)(2,1)}), bf16[4,64,2,1152]{3,1,2,0:T(8,128)(2,1)S(1)}, u32[]{:S(2)}, u32[]{:S(2)}) async-start(bf16[4,64,2,1152]{3,1,2,0:T(8,128)(2,1)} %copy.113), calls=%async_computation.4 | async-start | bytes 2359296 | tf_op jit(solution)/shard_map/all_to_all | solution.py:48
  305.9 27.1 %copy-start.8 = (bf16[1152,16]{0,1:T(8,128)(2,1)S(1)}, bf16[1152,16]{0,1:T(8,128)(2,1)}, u32[]{:S(2)}) copy-start(bf16[1152,16]{0,1:T(8,128)(2,1)} %param.27) | copy-start | bytes 110596
Sparse Core Ops, SparseCore 0:
  12.5 160.2 all-gather.7
  190.5 70.5 all-reduce.1
Sparse Core Ops, SparseCore 1:
  212.0 38.8 all-gather.9
  252.8 43.6 all-gather.11
where the time goes:
time: 343 us; the launch traced here: 342 us
  waiting for transfers between devices  183 us (53%)
  starting transfers between devices  45.4 us (13%)
  blocking collectives  43.3 us (13%)
  local copies, waits for them, and re-layouts  21.6 us (6%)
  matrix products  20.2 us (6%)
  between operations  17.8 us (5%)
  other arithmetic  10.3 us (3%)
    all_gather x1, waiting for transfers between devices, on_device(): lax.all_gather(qkv_weight, DP, axis=1, tiled=True)  51.8 us
    all_to_all x4, waiting for transfers between devices, from_everyone(): lax.all_to_all(jnp.broadcast_to(x[None], (size, *x.shape)), axis, 0, 0, t...  47.6 us
    all_gather x4, blocking collectives, gathered_by_axis(): x = lax.all_gather(x, axis, axis=dim, tiled=True)  43.3 us
    all_to_all x4, starting transfers between devices, from_everyone(): lax.all_to_all(jnp.broadcast_to(x[None], (size, *x.shape)), axis, 0, 0, t...  34.3 us
    all_gather x2, waiting for transfers between devices, gathered_by_axis(): x = lax.all_gather(x, axis, axis=dim, tiled=True)  25.5 us
    all_to_all x1, waiting for transfers between devices, sum_at_owner(): pieces = lax.all_to_all(cut_along(x, dim, size), axis, 0, 0, tiled=True)  24.8 us
    psum x1, waiting for transfers between devices, on_device(): lax.psum(attn_part.astype(jnp.bfloat16), 'mp').astype(jnp.float32)  21.1 us
    all_to_all x1, waiting for transfers between devices, on_device(): lax.all_to_all(summed.astype(jnp.bfloat16), DP, split_axis=0, concat_axis...  12.4 us
  transfers between devices with their start and end apart: 10, of which 8 were waited for; matrix products, arithmetic and copies ran while one was open for 8% of the time, Pallas kernels for 0%

commit v1 on v0

--- a/solution.py
+++ b/solution.py
@@ -130,7 +130,7 @@
     mixed = mixed.reshape(row_count, quarter)
     attn_part = jnp.dot(mixed, collect(proj_weight, DP, 1), preferred_element_type=jnp.float32)
     attn = (
-        lax.psum(attn_part.astype(jnp.bfloat16), "mp")
+        jnp.sum(lax.all_gather(attn_part.astype(jnp.bfloat16), "mp"), axis=0)
         .astype(jnp.float32)
         .reshape(image_count, tokens, width)
     )

time: 343 us -> 420 us (1.22)
  the two profiles are of different devices: /device:TPU:4 before, /device:TPU:2 now
where the time goes in v1:
time: 420 us; the launch traced here: 419 us
  waiting for transfers between devices  257 us (61%)
  blocking collectives  44.9 us (11%)
  starting transfers between devices  44.3 us (11%)
  local copies, waits for them, and re-layouts  21.6 us (5%)
  matrix products  20.1 us (5%)
  between operations  16.1 us (4%)
  other arithmetic  14.5 us (3%)
    all_gather x2, waiting for transfers between devices, gathered_by_axis(): x = lax.all_gather(x, axis, axis=dim, tiled=True)  78.3 us
    all_gather x1, waiting for transfers between devices, on_device(): lax.all_gather(qkv_weight, DP, axis=1, tiled=True)  51.7 us
    all_to_all x4, waiting for transfers between devices, from_everyone(): lax.all_to_all(jnp.broadcast_to(x[None], (size, *x.shape)), axis, 0, 0, t...  48.5 us
    all_gather x4, blocking collectives, gathered_by_axis(): x = lax.all_gather(x, axis, axis=dim, tiled=True)  44.9 us
    all_gather x1, waiting for transfers between devices, on_device(): lax.all_gather(attn_part.astype(jnp.bfloat16), 'mp')  41 us
    all_to_all x4, starting transfers between devices, from_everyone(): lax.all_to_all(jnp.broadcast_to(x[None], (size, *x.shape)), axis, 0, 0, t...  33.8 us
    all_to_all x1, waiting for transfers between devices, sum_at_owner(): pieces = lax.all_to_all(cut_along(x, dim, size), axis, 0, 0, tiled=True)  24.7 us
    all_to_all x1, waiting for transfers between devices, on_device(): lax.all_to_all(summed.astype(jnp.bfloat16), DP, split_axis=0, concat_axis...  13.3 us
  transfers between devices with their start and end apart: 10, of which 9 were waited for; matrix products, arithmetic and copies ran while one was open for 8% of the time, Pallas kernels for 0%

profile of v1, /device:TPU:2, one launch (start us, length us, event | category | flops | bytes accessed | tf_op | source)
XLA Modules:
  0.0 419.0 jit_solution(1821897589732077822)
XLA Ops:
  13.1 19.2 %all-to-all-start = ((bf16[64,2,288]{2,1,0:T(2,128)(2,1)}), bf16[64,2,288]{2,1,0:T(2,128)(2,1)S(1)}, u32[]{:S(2)}, u32[]{:S(2)}) async-start(bf16[64,2,288]{2,1,0:T(2,128)(2,1)} %broadcast_in_dim.50), calls=%async_computation | async-start | bytes 196608 | tf_op jit(solution)/shard_map/all_to_all | solution.py:15
  33.0 13.1 %all-to-all-done = bf16[64,2,288]{2,1,0:T(2,128)(2,1)S(1)} async-done(((bf16[64,2,288]{2,1,0:T(2,128)(2,1)}), bf16[64,2,288]{2,1,0:T(2,128)(2,1)S(1)}, u32[]{:S(2)}, u32[]{:S(2)}) %all-to-all-start) | async-done | bytes 73760 | tf_op jit(solution)/shard_map/all_to_all | solution.py:15
  48.0 4.6 %all-to-all-start.1 = ((bf16[4,128,108]{1,2,0:T(8,128)(2,1)}), bf16[4,128,108]{1,2,0:T(8,128)(2,1)S(1)}, u32[]{:S(2)}, u32[]{:S(2)}) async-start(bf16[4,128,108]{1,2,0:T(8,128)(2,1)} %broadcast_in_dim.84), calls=%async_computation.1 | async-start | bytes 229376 | tf_op jit(solution)/shard_map/all_to_all | solution.py:15
  53.9 4.5 %all-to-all-done.1 = bf16[4,128,108]{1,2,0:T(8,128)(2,1)S(1)} async-done(((bf16[4,128,108]{1,2,0:T(8,128)(2,1)}), bf16[4,128,108]{1,2,0:T(8,128)(2,1)S(1)}, u32[]{:S(2)}, u32[]{:S(2)}) %all-to-all-start.1) | async-done | bytes 110624 | tf_op jit(solution)/shard_map/all_to_all | solution.py:15
  59.1 5.4 %all-to-all-start.2 = ((bf16[64,2,108]{2,1,0:T(2,128)(2,1)}), bf16[64,2,108]{2,1,0:T(2,128)(2,1)S(1)}, u32[]{:S(2)}, u32[]{:S(2)}) async-start(bf16[64,2,108]{2,1,0:T(2,128)(2,1)} %bitcast.7), calls=%async_computation.2 | async-start | bytes 65536 | tf_op jit(solution)/shard_map/all_to_all | solution.py:100
  64.7 13.3 %all-to-all-done.2 = bf16[64,2,108]{2,1,0:T(2,128)(2,1)S(1)} async-done(((bf16[64,2,108]{2,1,0:T(2,128)(2,1)}), bf16[64,2,108]{2,1,0:T(2,128)(2,1)S(1)}, u32[]{:S(2)}, u32[]{:S(2)}) %all-to-all-start.2) | async-done | bytes 27680 | tf_op jit(solution)/shard_map/all_to_all | solution.py:100
  79.1 6.3 %all-to-all-start.3 = ((bf16[64,288,18]{1,2,0:T(8,128)(2,1)}), bf16[64,288,18]{1,2,0:T(8,128)(2,1)}, u32[]{:S(2)}, u32[]{:S(2)}) async-start(bf16[64,288,18]{1,2,0:T(8,128)(2,1)} %broadcast_in_dim.85), calls=%async_computation.3 | async-start | bytes 2359296 | tf_op jit(solution)/shard_map/all_to_all | solution.py:15
  86.2 1.7 fusion.16
  87.9 30.8 %all-to-all-done.3 = bf16[64,288,18]{1,2,0:T(8,128)(2,1)} async-done(((bf16[64,288,18]{1,2,0:T(8,128)(2,1)}), bf16[64,288,18]{1,2,0:T(8,128)(2,1)}, u32[]{:S(2)}, u32[]{:S(2)}) %all-to-all-start.3) | async-done | bytes 663584 | tf_op jit(solution)/shard_map/all_to_all | solution.py:15
  120.4 51.7 %all-gather.10.cloned.1.call-done = bf16[3,1152,288]{2,0,1:T(4,128)(2,1)} async-done(((bf16[3,18,288]{2,0,1:T(4,128)(2,1)}), bf16[3,1152,288]{2,0,1:T(4,128)(2,1)}) %all-gather.10.cloned.1.call-update) | async-done | bytes 1990672 | tf_op jit(solution)/shard_map/all_gather | solution.py:117
  172.1 3.7 fusion.26
  176.8 1.7 reshape_squeeze.10
  178.5 1.7 reshape_squeeze.11
  180.2 1.8 reshape_squeeze.9
  182.0 3.2 fusion.65
  185.2 2.0 fusion.30
  187.6 1.9 convolution_convert_fusion.2
  189.6 9.3 %all-gather.1 = bf16[2,18,1152]{2,1,0:T(8,128)(2,1)S(1)} all-gather(bf16[1,18,1152]{2,1,0:T(8,128)(2,1)S(1)} %bitcast.127), channel_id=1, replica_groups=mesh['group'=2,'dp_0'=8,'dp_1'=4,'dp_2'=2,'mp'=4] {'dp_2'}, dimensions={0}, use_global_device_ids=true | all-gather | bytes 124416 | tf_op jit(solution)/shard_map/all_gather | solution.py:36
  198.9 12.5 %all-gather.2 = bf16[4,36,1152]{2,1,0:T(8,128)(2,1)S(1)} all-gather(bf16[1,36,1152]{2,1,0:T(8,128)(2,1)S(1)} %reshape.325), channel_id=1, replica_groups=mesh['group'=2,'dp_0'=8,'dp_1'=4,'dp_2'=2,'mp'=4] {'dp_1'}, dimensions={0}, use_global_device_ids=true | all-gather | bytes 414720 | tf_op jit(solution)/shard_map/all_gather | solution.py:36
  212.3 10.6 %all-gather.3 = bf16[2,18,1152]{2,1,0:T(8,128)(2,1)S(1)} all-gather(bf16[1,18,1152]{2,1,0:T(8,128)(2,1)S(1)} %bitcast.128), channel_id=1, replica_groups=mesh['group'=2,'dp_0'=8,'dp_1'=4,'dp_2'=2,'mp'=4] {'dp_2'}, dimensions={0}, use_global_device_ids=true | all-gather | bytes 124416 | tf_op jit(solution)/shard_map/all_gather | solution.py:36
  222.9 12.5 %all-gather.4 = bf16[4,36,1152]{2,1,0:T(8,128)(2,1)S(1)} all-gather(bf16[1,36,1152]{2,1,0:T(8,128)(2,1)S(1)} %reshape.329), channel_id=1, replica_groups=mesh['group'=2,'dp_0'=8,'dp_1'=4,'dp_2'=2,'mp'=4] {'dp_1'}, dimensions={0}, use_global_device_ids=true | all-gather | bytes 414720 | tf_op jit(solution)/shard_map/all_gather | solution.py:36
  237.2 3.6 all-to-all-start.5
  240.8 41.0 %all-gather.16.cloned.1.call-done = bf16[2048,1152]{1,0:T(8,128)(2,1)} async-done(((bf16[512,1152]{1,0:T(8,128)(2,1)}), bf16[2048,1152]{1,0:T(8,128)(2,1)}) %all-gather.16.cloned.1.call-update) | async-done | bytes 4718608 | tf_op jit(solution)/shard_map/all_gather | solution.py:133
  281.8 4.4 %reduce_sum.109 = bf16[512,1152]{1,0:T(8,128)(2,1)} reduce(bf16[4,512,1152]{2,1,0:T(8,128)(2,1)} %bitcast.121, bf16[]{:T(256)} %constant.37.clone.1), dimensions={0}, to_apply=%region_5.6 | reduce | flops 1769472 | bytes 5898242 | tf_op jit(solution)/shard_map/reduce_sum | solution.py:133
  286.2 1.7 fusion.60
  290.0 1.9 fusion.12
  291.9 36.7 %all-gather.12.cloned.1.call-done = bf16[1152,1152]{1,0:T(8,128)(2,1)} async-done(((bf16[144,1152]{1,0:T(8,128)(2,1)}), bf16[1152,1152]{1,0:T(8,128)(2,1)}) %all-gather.12.cloned.1.call-update) | async-done | bytes 2654224 | tf_op jit(solution)/shard_map/all_gather | solution.py:36
  328.6 4.0 fusion.11
  332.6 41.6 %all-gather.14.cloned.1.call-done = bf16[1152,1152]{0,1:T(8,128)(2,1)} async-done(((bf16[1152,144]{0,1:T(8,128)(2,1)}), bf16[1152,1152]{0,1:T(8,128)(2,1)}) %all-gather.14.cloned.1.call-update) | async-done | bytes 2654224 | tf_op jit(solution)/shard_map/all_gather | solution.py:36
  374.2 3.6 convolution_convert_fusion.1
  379.0 5.1 %all-to-all-start.4 = ((bf16[4,64,2,1152]{3,1,2,0:T(8,128)(2,1)}), bf16[4,64,2,1152]{3,1,2,0:T(8,128)(2,1)S(1)}, u32[]{:S(2)}, u32[]{:S(2)}) async-start(bf16[4,64,2,1152]{3,1,2,0:T(8,128)(2,1)} %copy.113), calls=%async_computation.4 | async-start | bytes 2359296 | tf_op jit(solution)/shard_map/all_to_all | solution.py:48
  384.8 24.7 %all-to-all-done.4 = bf16[4,64,2,1152]{3,1,2,0:T(8,128)(2,1)S(1)} async-done(((bf16[4,64,2,1152]{3,1,2,0:T(8,128)(2,1)}), bf16[4,64,2,1152]{3,1,2,0:T(8,128)(2,1)S(1)}, u32[]{:S(2)}, u32[]{:S(2)}) %all-to-all-start.4) | async-done | bytes 1179680 | tf_op jit(solution)/shard_map/all_to_all | solution.py:48
  (84 shorter events, 23.0 us)
Async XLA Ops:
  6.5 229.7 %copy-start = (bf16[288,2304]{1,0:T(8,128)(2,1)S(1)}, bf16[288,2304]{1,0:T(8,128)(2,1)}, u32[]{:S(2)}) copy-start(bf16[288,2304]{1,0:T(8,128)(2,1)} %param.22) | copy-start | bytes 3981316
  6.5 165.5 %all-gather.10.cloned.1.call-start = ((), (), s32[]{:S(2)}) async-start(), calls=%async_computation.6 | async-start | bytes 3594240 | tf_op jit(solution)/shard_map/all_gather | solution.py:117
  11.8 0.6 copy-start.6
  13.1 64.9 %copy-start.5 = (bf16[288,18]{0,1:T(8,128)(2,1)S(1)}, bf16[288,18]{0,1:T(8,128)(2,1)}, u32[]{:S(2)}) copy-start(bf16[288,18]{0,1:T(8,128)(2,1)} %param.24) | copy-start | bytes 31108
  13.1 33.0 %all-to-all-start = ((bf16[64,2,288]{2,1,0:T(2,128)(2,1)}), bf16[64,2,288]{2,1,0:T(2,128)(2,1)S(1)}, u32[]{:S(2)}, u32[]{:S(2)}) async-start(bf16[64,2,288]{2,1,0:T(2,128)(2,1)} %broadcast_in_dim.50), calls=%async_computation | async-start | bytes 196608 | tf_op jit(solution)/shard_map/all_to_all | solution.py:15
  48.0 10.4 %all-to-all-start.1 = ((bf16[4,128,108]{1,2,0:T(8,128)(2,1)}), bf16[4,128,108]{1,2,0:T(8,128)(2,1)S(1)}, u32[]{:S(2)}, u32[]{:S(2)}) async-start(bf16[4,128,108]{1,2,0:T(8,128)(2,1)} %broadcast_in_dim.84), calls=%async_computation.1 | async-start | bytes 229376 | tf_op jit(solution)/shard_map/all_to_all | solution.py:15
  59.1 18.9 %all-to-all-start.2 = ((bf16[64,2,108]{2,1,0:T(2,128)(2,1)}), bf16[64,2,108]{2,1,0:T(2,128)(2,1)S(1)}, u32[]{:S(2)}, u32[]{:S(2)}) async-start(bf16[64,2,108]{2,1,0:T(2,128)(2,1)} %bitcast.7), calls=%async_computation.2 | async-start | bytes 65536 | tf_op jit(solution)/shard_map/all_to_all | solution.py:100
  79.1 39.6 %all-to-all-start.3 = ((bf16[64,288,18]{1,2,0:T(8,128)(2,1)}), bf16[64,288,18]{1,2,0:T(8,128)(2,1)}, u32[]{:S(2)}, u32[]{:S(2)}) async-start(bf16[64,288,18]{1,2,0:T(8,128)(2,1)} %broadcast_in_dim.85), calls=%async_computation.3 | async-start | bytes 2359296 | tf_op jit(solution)/shard_map/all_to_all | solution.py:15
  85.5 196.3 %all-gather.16.cloned.1.call-start = ((), (), s32[]{:S(2)}) async-start(), calls=%async_computation.9 | async-start | bytes 5898240 | tf_op jit(solution)/shard_map/all_gather | solution.py:133
  187.2 2.4 copy-start.3
  187.6 24.7 %copy-start.4 = (bf16[1152,18]{0,1:T(8,128)(2,1)S(1)}, bf16[1152,18]{0,1:T(8,128)(2,1)}, u32[]{:S(2)}) copy-start(bf16[1152,18]{0,1:T(8,128)(2,1)} %param.26) | copy-start | bytes 124420
  189.5 46.7 %copy-start.7 = (bf16[2,288]{1,0:T(2,128)(2,1)S(1)}, bf16[2,288]{1,0:T(2,128)(2,1)}, u32[]{:S(2)}) copy-start(bf16[2,288]{1,0:T(2,128)(2,1)} %copy-done.6) | copy-start | bytes 3460
  189.5 139.1 %all-gather.12.cloned.1.call-start = ((), (), s32[]{:S(2)}) async-start(), calls=%async_computation.7 | async-start | bytes 2985984 | tf_op jit(solution)/shard_map/all_gather | solution.py:36
  212.3 162.0 %all-gather.14.cloned.1.call-start = ((), (), s32[]{:S(2)}) async-start(), calls=%async_computation.8 | async-start | bytes 2985984 | tf_op jit(solution)/shard_map/all_gather | solution.py:36
  237.2 141.8 %all-to-all-start.5 = ((bf16[4,2,2304]{2,1,0:T(2,128)(2,1)}), bf16[4,2,2304]{2,1,0:T(2,128)(2,1)S(1)}, u32[]{:S(2)}, u32[]{:S(2)}) async-start(bf16[4,2,2304]{2,1,0:T(2,128)(2,1)} %broadcast_in_dim.86), calls=%async_computation.5 | async-start | bytes 73728 | tf_op jit(solution)/shard_map/all_to_all | solution.py:15
  287.9 1.4 copy-start.1
  287.9 2.1 copy-start.2
  379.0 30.5 %all-to-all-start.4 = ((bf16[4,64,2,1152]{3,1,2,0:T(8,128)(2,1)}), bf16[4,64,2,1152]{3,1,2,0:T(8,128)(2,1)S(1)}, u32[]{:S(2)}, u32[]{:S(2)}) async-start(bf16[4,64,2,1152]{3,1,2,0:T(8,128)(2,1)} %copy.113), calls=%async_computation.4 | async-start | bytes 2359296 | tf_op jit(solution)/shard_map/all_to_all | solution.py:48
  384.0 27.1 %copy-start.8 = (bf16[1152,16]{0,1:T(8,128)(2,1)S(1)}, bf16[1152,16]{0,1:T(8,128)(2,1)}, u32[]{:S(2)}) copy-start(bf16[1152,16]{0,1:T(8,128)(2,1)} %param.27) | copy-start | bytes 110596
Sparse Core Ops, SparseCore 0:
  11.7 160.3 all-gather.9
  189.7 92.1 all-gather.15
  283.9 44.6 all-gather.11
  330.5 43.6 all-gather.13
